TPU v7x, 32 devices: a whole 2x2x4 slice. The times are simulated.
32 devices in a mesh: dp: 2 (over x), fsdp: 16 (over z, y, core).
Axes of the slice: x: 2, y: 2, z: 4, core: 2. Of those that a mesh axis runs over, the one named last changes fastest.
Arguments:
- hidden: bfloat16 [2, 16384, 512], P(None, ('dp', 'fsdp')), parts along dimension 1
- targets: int32 [2, 16384], P(None, ('dp', 'fsdp')), parts along dimension 1
- w_out: bfloat16 [32128, 512], P('fsdp')
Outputs:
- output 1: float32 [4], P('dp'), parts along dimension 0
- output 2: float32 [2, 16384, 512], P(None, ('dp', 'fsdp')), parts along dimension 1
- output 3: float32 [64256, 512], P(('dp', 'fsdp')), parts along dimension 0
There are 2 independent parts. A program takes and returns all parts, laid end to end along the dimension named above; an argument that names none is the same for every part.
All inputs are finite; a program needn't handle non-finite values.
Results may differ from a plain program's by a relative error of at most 0.001.
Values are sent between devices in bfloat16 or wider.
A program may use at most 1 GiB of HBM per device.

v0:
```python
import jax
import jax.numpy as jnp
from jax import lax
from jax.sharding import PartitionSpec as P


def solution(mesh):
    group_size = mesh.shape['fsdp']
    shift_perm = [(src_idx, (src_idx - 1) % group_size) for src_idx in range(group_size)]

    def local_head(hidden, targets, w_loc):
        n_micro, tok_dev, model_dim = hidden.shape
        blk_rows = w_loc.shape[0]
        tokens = tok_dev * group_size
        n_rows = n_micro * tok_dev
        tok_rows = hidden.reshape(n_rows, model_dim)
        row_tgt = targets.reshape(n_rows)
        col_ids = lax.broadcasted_iota(jnp.int32, (1, blk_rows), 1)
        my_idx = lax.axis_index('fsdp')

        def block_logits(w_blk, step_idx):
            blk_idx = (my_idx + step_idx) % group_size
            logits = lax.dot_general(tok_rows, w_blk, (((1,), (1,)), ((), ())), preferred_element_type=jnp.float32)
            tgt_hit = (row_tgt - blk_idx * blk_rows)[:, None] == col_ids
            return logits, tgt_hit

        def fwd_update(run_stats, w_blk, step_idx):
            run_max, run_sum, tgt_logit = run_stats
            logits, tgt_hit = block_logits(w_blk, step_idx)
            tgt_logit = tgt_logit + jnp.sum(jnp.where(tgt_hit, logits, 0.0), axis=1)
            new_max = jnp.maximum(run_max, jnp.max(logits, axis=1))
            run_sum = run_sum * jnp.exp(run_max - new_max) + jnp.sum(jnp.exp(logits - new_max[:, None]), axis=1)
            return new_max, run_sum, tgt_logit

        init_stats = (jnp.full((n_rows,), -jnp.inf, jnp.float32), jnp.zeros((n_rows,), jnp.float32), jnp.zeros((n_rows,), jnp.float32))
        first_stats = fwd_update(init_stats, w_loc, 0)

        def fwd_body(step_idx, loop_carry):
            w_cur, run_stats = loop_carry
            w_cur = lax.ppermute(w_cur, 'fsdp', shift_perm)
            return w_cur, fwd_update(run_stats, w_cur, step_idx)

        _, (run_max, run_sum, tgt_logit) = lax.fori_loop(1, group_size, fwd_body, (w_loc, first_stats))
        log_norm = run_max + jnp.log(run_sum)
        loss_vals = lax.psum(jnp.sum((log_norm - tgt_logit).reshape(n_micro, tok_dev), axis=1) / tokens, 'fsdp')

        def bwd_update(d_rows, w_blk, step_idx):
            logits, tgt_hit = block_logits(w_blk, step_idx)
            soft_probs = jnp.exp(logits - log_norm[:, None])
            d_logits = ((soft_probs - tgt_hit.astype(jnp.float32)) / tokens).astype(jnp.bfloat16)
            d_rows = d_rows + jnp.dot(d_logits, w_blk, preferred_element_type=jnp.float32)
            d_w_part = lax.dot_general(d_logits, tok_rows, (((0,), (0,)), ((), ())), preferred_element_type=jnp.float32)
            return d_rows, d_w_part

        d_rows, d_w_acc = bwd_update(jnp.zeros((n_rows, model_dim), jnp.float32), w_loc, 0)

        def bwd_body(step_idx, loop_carry):
            w_cur, d_w_acc, d_rows = loop_carry
            w_cur = lax.ppermute(w_cur, 'fsdp', shift_perm)
            d_w_acc = lax.ppermute(d_w_acc, 'fsdp', shift_perm)
            d_rows, d_w_part = bwd_update(d_rows, w_cur, step_idx)
            return w_cur, d_w_acc + d_w_part, d_rows

        _, d_w_acc, d_rows = lax.fori_loop(1, group_size, bwd_body, (w_loc, d_w_acc, d_rows))
        d_w = lax.ppermute(d_w_acc, 'fsdp', shift_perm)
        return loss_vals, d_rows.reshape(n_micro, tok_dev, model_dim), d_w

    return jax.shard_map(local_head, mesh=mesh,
                         in_specs=(P(None, ('dp', 'fsdp'), None), P(None, ('dp', 'fsdp')), P('fsdp', None)),
                         out_specs=(P('dp'), P(None, ('dp', 'fsdp'), None), P(('dp', 'fsdp'), None)),
                         check_vma=False)
```

profile of v0, /device:TPU:0, one launch (start us, length us, event | category | flops | bytes accessed | tf_op | source)
XLA Modules:
  0.0 1910.5 jit_solution(16914979716388144752)
XLA Ops:
  13.7 507.3 %while.42 = (s32[]{:T(128)}, bf16[2008,512]{1,0:T(8,128)(2,1)}, f32[1024]{0:T(1024)S(1)}, f32[1024]{0:T(1024)S(1)}, f32[1024]{0:T(1024)S(1)}, /*index=5*/bf16[10...) while((s32[]{:T(128)}, bf16[2008,512]{1,0:T(8,128)(2,1)}, ...), condition=%wide.region_7.8_spmd.clone, body=%wide.region_3.7_spmd.clone.sunk | while | flops 2117880832 | bytes 31973672 | solution.py:43
  19.3 23.1 %collective-permute-done = bf16[2008,512]{1,0:T(8,128)(2,1)S(1)} collective-permute-done((bf16[2008,512]{1,0:T(8,128)(2,1)}, bf16[2008,512]{1,0:T(8,128)(2,1)S(1)}, u32[]{:S(2)}, u32[]{:S(2)}) %collective-permute-start) | collective-permute-done | bytes 2056224 | tf_op jit(solution)/shard_map/while/body/eval_jaxpr/ppermute | solution.py:40
  53.1 23.1 %collective-permute-done = bf16[2008,512]{1,0:T(8,128)(2,1)S(1)} collective-permute-done((bf16[2008,512]{1,0:T(8,128)(2,1)}, bf16[2008,512]{1,0:T(8,128)(2,1)S(1)}, u32[]{:S(2)}, u32[]{:S(2)}) %collective-permute-start) | collective-permute-done | bytes 2056224 | tf_op jit(solution)/shard_map/while/body/eval_jaxpr/ppermute | solution.py:40
  86.8 23.1 %collective-permute-done = bf16[2008,512]{1,0:T(8,128)(2,1)S(1)} collective-permute-done((bf16[2008,512]{1,0:T(8,128)(2,1)}, bf16[2008,512]{1,0:T(8,128)(2,1)S(1)}, u32[]{:S(2)}, u32[]{:S(2)}) %collective-permute-start) | collective-permute-done | bytes 2056224 | tf_op jit(solution)/shard_map/while/body/eval_jaxpr/ppermute | solution.py:40
  120.6 23.1 %collective-permute-done = bf16[2008,512]{1,0:T(8,128)(2,1)S(1)} collective-permute-done((bf16[2008,512]{1,0:T(8,128)(2,1)}, bf16[2008,512]{1,0:T(8,128)(2,1)S(1)}, u32[]{:S(2)}, u32[]{:S(2)}) %collective-permute-start) | collective-permute-done | bytes 2056224 | tf_op jit(solution)/shard_map/while/body/eval_jaxpr/ppermute | solution.py:40
  154.3 23.1 %collective-permute-done = bf16[2008,512]{1,0:T(8,128)(2,1)S(1)} collective-permute-done((bf16[2008,512]{1,0:T(8,128)(2,1)}, bf16[2008,512]{1,0:T(8,128)(2,1)S(1)}, u32[]{:S(2)}, u32[]{:S(2)}) %collective-permute-start) | collective-permute-done | bytes 2056224 | tf_op jit(solution)/shard_map/while/body/eval_jaxpr/ppermute | solution.py:40
  188.1 23.1 %collective-permute-done = bf16[2008,512]{1,0:T(8,128)(2,1)S(1)} collective-permute-done((bf16[2008,512]{1,0:T(8,128)(2,1)}, bf16[2008,512]{1,0:T(8,128)(2,1)S(1)}, u32[]{:S(2)}, u32[]{:S(2)}) %collective-permute-start) | collective-permute-done | bytes 2056224 | tf_op jit(solution)/shard_map/while/body/eval_jaxpr/ppermute | solution.py:40
  221.8 23.1 %collective-permute-done = bf16[2008,512]{1,0:T(8,128)(2,1)S(1)} collective-permute-done((bf16[2008,512]{1,0:T(8,128)(2,1)}, bf16[2008,512]{1,0:T(8,128)(2,1)S(1)}, u32[]{:S(2)}, u32[]{:S(2)}) %collective-permute-start) | collective-permute-done | bytes 2056224 | tf_op jit(solution)/shard_map/while/body/eval_jaxpr/ppermute | solution.py:40
  255.6 23.1 %collective-permute-done = bf16[2008,512]{1,0:T(8,128)(2,1)S(1)} collective-permute-done((bf16[2008,512]{1,0:T(8,128)(2,1)}, bf16[2008,512]{1,0:T(8,128)(2,1)S(1)}, u32[]{:S(2)}, u32[]{:S(2)}) %collective-permute-start) | collective-permute-done | bytes 2056224 | tf_op jit(solution)/shard_map/while/body/eval_jaxpr/ppermute | solution.py:40
  289.3 23.1 %collective-permute-done = bf16[2008,512]{1,0:T(8,128)(2,1)S(1)} collective-permute-done((bf16[2008,512]{1,0:T(8,128)(2,1)}, bf16[2008,512]{1,0:T(8,128)(2,1)S(1)}, u32[]{:S(2)}, u32[]{:S(2)}) %collective-permute-start) | collective-permute-done | bytes 2056224 | tf_op jit(solution)/shard_map/while/body/eval_jaxpr/ppermute | solution.py:40
  323.1 23.1 %collective-permute-done = bf16[2008,512]{1,0:T(8,128)(2,1)S(1)} collective-permute-done((bf16[2008,512]{1,0:T(8,128)(2,1)}, bf16[2008,512]{1,0:T(8,128)(2,1)S(1)}, u32[]{:S(2)}, u32[]{:S(2)}) %collective-permute-start) | collective-permute-done | bytes 2056224 | tf_op jit(solution)/shard_map/while/body/eval_jaxpr/ppermute | solution.py:40
  356.9 23.1 %collective-permute-done = bf16[2008,512]{1,0:T(8,128)(2,1)S(1)} collective-permute-done((bf16[2008,512]{1,0:T(8,128)(2,1)}, bf16[2008,512]{1,0:T(8,128)(2,1)S(1)}, u32[]{:S(2)}, u32[]{:S(2)}) %collective-permute-start) | collective-permute-done | bytes 2056224 | tf_op jit(solution)/shard_map/while/body/eval_jaxpr/ppermute | solution.py:40
  390.6 23.1 %collective-permute-done = bf16[2008,512]{1,0:T(8,128)(2,1)S(1)} collective-permute-done((bf16[2008,512]{1,0:T(8,128)(2,1)}, bf16[2008,512]{1,0:T(8,128)(2,1)S(1)}, u32[]{:S(2)}, u32[]{:S(2)}) %collective-permute-start) | collective-permute-done | bytes 2056224 | tf_op jit(solution)/shard_map/while/body/eval_jaxpr/ppermute | solution.py:40
  424.4 23.1 %collective-permute-done = bf16[2008,512]{1,0:T(8,128)(2,1)S(1)} collective-permute-done((bf16[2008,512]{1,0:T(8,128)(2,1)}, bf16[2008,512]{1,0:T(8,128)(2,1)S(1)}, u32[]{:S(2)}, u32[]{:S(2)}) %collective-permute-start) | collective-permute-done | bytes 2056224 | tf_op jit(solution)/shard_map/while/body/eval_jaxpr/ppermute | solution.py:40
  458.1 23.1 %collective-permute-done = bf16[2008,512]{1,0:T(8,128)(2,1)S(1)} collective-permute-done((bf16[2008,512]{1,0:T(8,128)(2,1)}, bf16[2008,512]{1,0:T(8,128)(2,1)S(1)}, u32[]{:S(2)}, u32[]{:S(2)}) %collective-permute-start) | collective-permute-done | bytes 2056224 | tf_op jit(solution)/shard_map/while/body/eval_jaxpr/ppermute | solution.py:40
  491.9 23.1 %collective-permute-done = bf16[2008,512]{1,0:T(8,128)(2,1)S(1)} collective-permute-done((bf16[2008,512]{1,0:T(8,128)(2,1)}, bf16[2008,512]{1,0:T(8,128)(2,1)S(1)}, u32[]{:S(2)}, u32[]{:S(2)}) %collective-permute-start) | collective-permute-done | bytes 2056224 | tf_op jit(solution)/shard_map/while/body/eval_jaxpr/ppermute | solution.py:40
  521.0 7.8 fusion.4
  533.5 1295.0 %while.43 = (s32[]{:T(128)}, bf16[2008,512]{1,0:T(8,128)(2,1)}, f32[2008,512]{1,0:T(8,128)}, f32[1024,512]{1,0:T(8,128)}, bf16[1024,512]{1,0:T(8,128)(2,1)S(1)},...) while((s32[]{:T(128)}, bf16[2008,512]{1,0:T(8,128)(2,1)}, ...), condition=%wide.region_11.12_spmd.clone, body=%wide.region_10.11_spmd.clone.sunk | while | flops 6330512384 | bytes 76546440 | solution.py:64
  538.2 67.1 %collective-permute-done.1 = bf16[2008,512]{1,0:T(8,128)(2,1)S(1)} collective-permute-done((bf16[2008,512]{1,0:T(8,128)(2,1)}, bf16[2008,512]{1,0:T(8,128)(2,1)S(1)}, u32[]{:S(2)}, u32[]{:S(2)}) %collective-permute-start.1) | collective-permute-done | bytes 2056224 | tf_op jit(solution)/shard_map/while/body/eval_jaxpr/ppermute | solution.py:59
  612.6 7.2 convolution_add_fusion.4
  624.5 67.1 %collective-permute-done.1 = bf16[2008,512]{1,0:T(8,128)(2,1)S(1)} collective-permute-done((bf16[2008,512]{1,0:T(8,128)(2,1)}, bf16[2008,512]{1,0:T(8,128)(2,1)S(1)}, u32[]{:S(2)}, u32[]{:S(2)}) %collective-permute-start.1) | collective-permute-done | bytes 2056224 | tf_op jit(solution)/shard_map/while/body/eval_jaxpr/ppermute | solution.py:59
  698.9 7.2 convolution_add_fusion.4
  710.8 67.1 %collective-permute-done.1 = bf16[2008,512]{1,0:T(8,128)(2,1)S(1)} collective-permute-done((bf16[2008,512]{1,0:T(8,128)(2,1)}, bf16[2008,512]{1,0:T(8,128)(2,1)S(1)}, u32[]{:S(2)}, u32[]{:S(2)}) %collective-permute-start.1) | collective-permute-done | bytes 2056224 | tf_op jit(solution)/shard_map/while/body/eval_jaxpr/ppermute | solution.py:59
  785.3 7.2 convolution_add_fusion.4
  797.2 67.1 %collective-permute-done.1 = bf16[2008,512]{1,0:T(8,128)(2,1)S(1)} collective-permute-done((bf16[2008,512]{1,0:T(8,128)(2,1)}, bf16[2008,512]{1,0:T(8,128)(2,1)S(1)}, u32[]{:S(2)}, u32[]{:S(2)}) %collective-permute-start.1) | collective-permute-done | bytes 2056224 | tf_op jit(solution)/shard_map/while/body/eval_jaxpr/ppermute | solution.py:59
  871.6 7.2 convolution_add_fusion.4
  883.5 67.1 %collective-permute-done.1 = bf16[2008,512]{1,0:T(8,128)(2,1)S(1)} collective-permute-done((bf16[2008,512]{1,0:T(8,128)(2,1)}, bf16[2008,512]{1,0:T(8,128)(2,1)S(1)}, u32[]{:S(2)}, u32[]{:S(2)}) %collective-permute-start.1) | collective-permute-done | bytes 2056224 | tf_op jit(solution)/shard_map/while/body/eval_jaxpr/ppermute | solution.py:59
  957.9 7.2 convolution_add_fusion.4
  969.8 67.1 %collective-permute-done.1 = bf16[2008,512]{1,0:T(8,128)(2,1)S(1)} collective-permute-done((bf16[2008,512]{1,0:T(8,128)(2,1)}, bf16[2008,512]{1,0:T(8,128)(2,1)S(1)}, u32[]{:S(2)}, u32[]{:S(2)}) %collective-permute-start.1) | collective-permute-done | bytes 2056224 | tf_op jit(solution)/shard_map/while/body/eval_jaxpr/ppermute | solution.py:59
  1044.3 7.2 convolution_add_fusion.4
  1056.2 67.1 %collective-permute-done.1 = bf16[2008,512]{1,0:T(8,128)(2,1)S(1)} collective-permute-done((bf16[2008,512]{1,0:T(8,128)(2,1)}, bf16[2008,512]{1,0:T(8,128)(2,1)S(1)}, u32[]{:S(2)}, u32[]{:S(2)}) %collective-permute-start.1) | collective-permute-done | bytes 2056224 | tf_op jit(solution)/shard_map/while/body/eval_jaxpr/ppermute | solution.py:59
  1130.6 7.2 convolution_add_fusion.4
  1142.5 67.1 %collective-permute-done.1 = bf16[2008,512]{1,0:T(8,128)(2,1)S(1)} collective-permute-done((bf16[2008,512]{1,0:T(8,128)(2,1)}, bf16[2008,512]{1,0:T(8,128)(2,1)S(1)}, u32[]{:S(2)}, u32[]{:S(2)}) %collective-permute-start.1) | collective-permute-done | bytes 2056224 | tf_op jit(solution)/shard_map/while/body/eval_jaxpr/ppermute | solution.py:59
  1216.9 7.2 convolution_add_fusion.4
  1228.8 67.1 %collective-permute-done.1 = bf16[2008,512]{1,0:T(8,128)(2,1)S(1)} collective-permute-done((bf16[2008,512]{1,0:T(8,128)(2,1)}, bf16[2008,512]{1,0:T(8,128)(2,1)S(1)}, u32[]{:S(2)}, u32[]{:S(2)}) %collective-permute-start.1) | collective-permute-done | bytes 2056224 | tf_op jit(solution)/shard_map/while/body/eval_jaxpr/ppermute | solution.py:59
  1303.3 7.2 convolution_add_fusion.4
  1315.2 67.1 %collective-permute-done.1 = bf16[2008,512]{1,0:T(8,128)(2,1)S(1)} collective-permute-done((bf16[2008,512]{1,0:T(8,128)(2,1)}, bf16[2008,512]{1,0:T(8,128)(2,1)S(1)}, u32[]{:S(2)}, u32[]{:S(2)}) %collective-permute-start.1) | collective-permute-done | bytes 2056224 | tf_op jit(solution)/shard_map/while/body/eval_jaxpr/ppermute | solution.py:59
  1389.6 7.2 convolution_add_fusion.4
  1401.5 67.1 %collective-permute-done.1 = bf16[2008,512]{1,0:T(8,128)(2,1)S(1)} collective-permute-done((bf16[2008,512]{1,0:T(8,128)(2,1)}, bf16[2008,512]{1,0:T(8,128)(2,1)S(1)}, u32[]{:S(2)}, u32[]{:S(2)}) %collective-permute-start.1) | collective-permute-done | bytes 2056224 | tf_op jit(solution)/shard_map/while/body/eval_jaxpr/ppermute | solution.py:59
  1475.9 7.2 convolution_add_fusion.4
  1487.8 67.1 %collective-permute-done.1 = bf16[2008,512]{1,0:T(8,128)(2,1)S(1)} collective-permute-done((bf16[2008,512]{1,0:T(8,128)(2,1)}, bf16[2008,512]{1,0:T(8,128)(2,1)S(1)}, u32[]{:S(2)}, u32[]{:S(2)}) %collective-permute-start.1) | collective-permute-done | bytes 2056224 | tf_op jit(solution)/shard_map/while/body/eval_jaxpr/ppermute | solution.py:59
  1562.3 7.2 convolution_add_fusion.4
  1574.2 67.1 %collective-permute-done.1 = bf16[2008,512]{1,0:T(8,128)(2,1)S(1)} collective-permute-done((bf16[2008,512]{1,0:T(8,128)(2,1)}, bf16[2008,512]{1,0:T(8,128)(2,1)S(1)}, u32[]{:S(2)}, u32[]{:S(2)}) %collective-permute-start.1) | collective-permute-done | bytes 2056224 | tf_op jit(solution)/shard_map/while/body/eval_jaxpr/ppermute | solution.py:59
  1648.6 7.2 convolution_add_fusion.4
  1660.5 67.1 %collective-permute-done.1 = bf16[2008,512]{1,0:T(8,128)(2,1)S(1)} collective-permute-done((bf16[2008,512]{1,0:T(8,128)(2,1)}, bf16[2008,512]{1,0:T(8,128)(2,1)S(1)}, u32[]{:S(2)}, u32[]{:S(2)}) %collective-permute-start.1) | collective-permute-done | bytes 2056224 | tf_op jit(solution)/shard_map/while/body/eval_jaxpr/ppermute | solution.py:59
  1734.9 7.2 convolution_add_fusion.4
  1746.8 67.2 %collective-permute-done.1 = bf16[2008,512]{1,0:T(8,128)(2,1)S(1)} collective-permute-done((bf16[2008,512]{1,0:T(8,128)(2,1)}, bf16[2008,512]{1,0:T(8,128)(2,1)S(1)}, u32[]{:S(2)}, u32[]{:S(2)}) %collective-permute-start.1) | collective-permute-done | bytes 2056224 | tf_op jit(solution)/shard_map/while/body/eval_jaxpr/ppermute | solution.py:59
  1833.3 72.7 %psum.7 = f32[2]{0:T(128)} all-reduce(f32[2]{0:T(128)S(1)} %broadcast_multiply_fusion), channel_id=1, replica_groups=mesh['dp'=2,'fsdp'=16] {'fsdp'}, use_global_device_ids=true, to_apply=%region_9.10 | all-reduce | flops 2 | bytes 16 | tf_op jit(solution)/shard_map/psum | solution.py:45
  (324 shorter events, 373.9 us)
Async XLA Ops:
  13.7 28.7 %collective-permute-start = (bf16[2008,512]{1,0:T(8,128)(2,1)}, bf16[2008,512]{1,0:T(8,128)(2,1)S(1)}, u32[]{:S(2)}, u32[]{:S(2)}) collective-permute-start(bf16[2008,512]{1,0:T(8,128)(2,1)} %get-tuple-element.651), channel_id=1, source_target_pairs={{0,15},{1,0},{2,1},{3,2},{4,3},{5,4},{6,5},{7,6},{8,7},{9,8},{10,9... | collective-permute-start | bytes 6168584 | tf_op jit(solution)/shard_map/while/body/eval_jaxpr/ppermute | solution.py:40
  48.4 27.7 %collective-permute-start = (bf16[2008,512]{1,0:T(8,128)(2,1)}, bf16[2008,512]{1,0:T(8,128)(2,1)S(1)}, u32[]{:S(2)}, u32[]{:S(2)}) collective-permute-start(bf16[2008,512]{1,0:T(8,128)(2,1)} %get-tuple-element.651), channel_id=1, source_target_pairs={{0,15},{1,0},{2,1},{3,2},{4,3},{5,4},{6,5},{7,6},{8,7},{9,8},{10,9... | collective-permute-start | bytes 6168584 | tf_op jit(solution)/shard_map/while/body/eval_jaxpr/ppermute | solution.py:40
  82.2 27.7 %collective-permute-start = (bf16[2008,512]{1,0:T(8,128)(2,1)}, bf16[2008,512]{1,0:T(8,128)(2,1)S(1)}, u32[]{:S(2)}, u32[]{:S(2)}) collective-permute-start(bf16[2008,512]{1,0:T(8,128)(2,1)} %get-tuple-element.651), channel_id=1, source_target_pairs={{0,15},{1,0},{2,1},{3,2},{4,3},{5,4},{6,5},{7,6},{8,7},{9,8},{10,9... | collective-permute-start | bytes 6168584 | tf_op jit(solution)/shard_map/while/body/eval_jaxpr/ppermute | solution.py:40
  115.9 27.7 %collective-permute-start = (bf16[2008,512]{1,0:T(8,128)(2,1)}, bf16[2008,512]{1,0:T(8,128)(2,1)S(1)}, u32[]{:S(2)}, u32[]{:S(2)}) collective-permute-start(bf16[2008,512]{1,0:T(8,128)(2,1)} %get-tuple-element.651), channel_id=1, source_target_pairs={{0,15},{1,0},{2,1},{3,2},{4,3},{5,4},{6,5},{7,6},{8,7},{9,8},{10,9... | collective-permute-start | bytes 6168584 | tf_op jit(solution)/shard_map/while/body/eval_jaxpr/ppermute | solution.py:40
  149.7 27.7 %collective-permute-start = (bf16[2008,512]{1,0:T(8,128)(2,1)}, bf16[2008,512]{1,0:T(8,128)(2,1)S(1)}, u32[]{:S(2)}, u32[]{:S(2)}) collective-permute-start(bf16[2008,512]{1,0:T(8,128)(2,1)} %get-tuple-element.651), channel_id=1, source_target_pairs={{0,15},{1,0},{2,1},{3,2},{4,3},{5,4},{6,5},{7,6},{8,7},{9,8},{10,9... | collective-permute-start | bytes 6168584 | tf_op jit(solution)/shard_map/while/body/eval_jaxpr/ppermute | solution.py:40
  183.5 27.7 %collective-permute-start = (bf16[2008,512]{1,0:T(8,128)(2,1)}, bf16[2008,512]{1,0:T(8,128)(2,1)S(1)}, u32[]{:S(2)}, u32[]{:S(2)}) collective-permute-start(bf16[2008,512]{1,0:T(8,128)(2,1)} %get-tuple-element.651), channel_id=1, source_target_pairs={{0,15},{1,0},{2,1},{3,2},{4,3},{5,4},{6,5},{7,6},{8,7},{9,8},{10,9... | collective-permute-start | bytes 6168584 | tf_op jit(solution)/shard_map/while/body/eval_jaxpr/ppermute | solution.py:40
  217.2 27.7 %collective-permute-start = (bf16[2008,512]{1,0:T(8,128)(2,1)}, bf16[2008,512]{1,0:T(8,128)(2,1)S(1)}, u32[]{:S(2)}, u32[]{:S(2)}) collective-permute-start(bf16[2008,512]{1,0:T(8,128)(2,1)} %get-tuple-element.651), channel_id=1, source_target_pairs={{0,15},{1,0},{2,1},{3,2},{4,3},{5,4},{6,5},{7,6},{8,7},{9,8},{10,9... | collective-permute-start | bytes 6168584 | tf_op jit(solution)/shard_map/while/body/eval_jaxpr/ppermute | solution.py:40
  251.0 27.7 %collective-permute-start = (bf16[2008,512]{1,0:T(8,128)(2,1)}, bf16[2008,512]{1,0:T(8,128)(2,1)S(1)}, u32[]{:S(2)}, u32[]{:S(2)}) collective-permute-start(bf16[2008,512]{1,0:T(8,128)(2,1)} %get-tuple-element.651), channel_id=1, source_target_pairs={{0,15},{1,0},{2,1},{3,2},{4,3},{5,4},{6,5},{7,6},{8,7},{9,8},{10,9... | collective-permute-start | bytes 6168584 | tf_op jit(solution)/shard_map/while/body/eval_jaxpr/ppermute | solution.py:40
  284.7 27.7 %collective-permute-start = (bf16[2008,512]{1,0:T(8,128)(2,1)}, bf16[2008,512]{1,0:T(8,128)(2,1)S(1)}, u32[]{:S(2)}, u32[]{:S(2)}) collective-permute-start(bf16[2008,512]{1,0:T(8,128)(2,1)} %get-tuple-element.651), channel_id=1, source_target_pairs={{0,15},{1,0},{2,1},{3,2},{4,3},{5,4},{6,5},{7,6},{8,7},{9,8},{10,9... | collective-permute-start | bytes 6168584 | tf_op jit(solution)/shard_map/while/body/eval_jaxpr/ppermute | solution.py:40
  318.5 27.7 %collective-permute-start = (bf16[2008,512]{1,0:T(8,128)(2,1)}, bf16[2008,512]{1,0:T(8,128)(2,1)S(1)}, u32[]{:S(2)}, u32[]{:S(2)}) collective-permute-start(bf16[2008,512]{1,0:T(8,128)(2,1)} %get-tuple-element.651), channel_id=1, source_target_pairs={{0,15},{1,0},{2,1},{3,2},{4,3},{5,4},{6,5},{7,6},{8,7},{9,8},{10,9... | collective-permute-start | bytes 6168584 | tf_op jit(solution)/shard_map/while/body/eval_jaxpr/ppermute | solution.py:40
  352.2 27.7 %collective-permute-start = (bf16[2008,512]{1,0:T(8,128)(2,1)}, bf16[2008,512]{1,0:T(8,128)(2,1)S(1)}, u32[]{:S(2)}, u32[]{:S(2)}) collective-permute-start(bf16[2008,512]{1,0:T(8,128)(2,1)} %get-tuple-element.651), channel_id=1, source_target_pairs={{0,15},{1,0},{2,1},{3,2},{4,3},{5,4},{6,5},{7,6},{8,7},{9,8},{10,9... | collective-permute-start | bytes 6168584 | tf_op jit(solution)/shard_map/while/body/eval_jaxpr/ppermute | solution.py:40
  386.0 27.7 %collective-permute-start = (bf16[2008,512]{1,0:T(8,128)(2,1)}, bf16[2008,512]{1,0:T(8,128)(2,1)S(1)}, u32[]{:S(2)}, u32[]{:S(2)}) collective-permute-start(bf16[2008,512]{1,0:T(8,128)(2,1)} %get-tuple-element.651), channel_id=1, source_target_pairs={{0,15},{1,0},{2,1},{3,2},{4,3},{5,4},{6,5},{7,6},{8,7},{9,8},{10,9... | collective-permute-start | bytes 6168584 | tf_op jit(solution)/shard_map/while/body/eval_jaxpr/ppermute | solution.py:40
  419.7 27.7 %collective-permute-start = (bf16[2008,512]{1,0:T(8,128)(2,1)}, bf16[2008,512]{1,0:T(8,128)(2,1)S(1)}, u32[]{:S(2)}, u32[]{:S(2)}) collective-permute-start(bf16[2008,512]{1,0:T(8,128)(2,1)} %get-tuple-element.651), channel_id=1, source_target_pairs={{0,15},{1,0},{2,1},{3,2},{4,3},{5,4},{6,5},{7,6},{8,7},{9,8},{10,9... | collective-permute-start | bytes 6168584 | tf_op jit(solution)/shard_map/while/body/eval_jaxpr/ppermute | solution.py:40
  453.5 27.7 %collective-permute-start = (bf16[2008,512]{1,0:T(8,128)(2,1)}, bf16[2008,512]{1,0:T(8,128)(2,1)S(1)}, u32[]{:S(2)}, u32[]{:S(2)}) collective-permute-start(bf16[2008,512]{1,0:T(8,128)(2,1)} %get-tuple-element.651), channel_id=1, source_target_pairs={{0,15},{1,0},{2,1},{3,2},{4,3},{5,4},{6,5},{7,6},{8,7},{9,8},{10,9... | collective-permute-start | bytes 6168584 | tf_op jit(solution)/shard_map/while/body/eval_jaxpr/ppermute | solution.py:40
  487.3 27.7 %collective-permute-start = (bf16[2008,512]{1,0:T(8,128)(2,1)}, bf16[2008,512]{1,0:T(8,128)(2,1)S(1)}, u32[]{:S(2)}, u32[]{:S(2)}) collective-permute-start(bf16[2008,512]{1,0:T(8,128)(2,1)} %get-tuple-element.651), channel_id=1, source_target_pairs={{0,15},{1,0},{2,1},{3,2},{4,3},{5,4},{6,5},{7,6},{8,7},{9,8},{10,9... | collective-permute-start | bytes 6168584 | tf_op jit(solution)/shard_map/while/body/eval_jaxpr/ppermute | solution.py:40
  521.0 7.8 copy-start
  533.5 79.1 %collective-permute-start.2 = (f32[2008,512]{1,0:T(8,128)}, f32[2008,512]{1,0:T(8,128)}, u32[]{:S(2)}, u32[]{:S(2)}) collective-permute-start(f32[2008,512]{1,0:T(8,128)} %get-tuple-element.691), channel_id=1, source_target_pairs={{0,15},{1,0},{2,1},{3,2},{4,3},{5,4},{6,5},{7,6},{8,7},{9,8},{10,9... | collective-permute-start | bytes 12337160 | tf_op jit(solution)/shard_map/while/body/eval_jaxpr/ppermute | solution.py:60
  538.1 67.2 %collective-permute-start.1 = (bf16[2008,512]{1,0:T(8,128)(2,1)}, bf16[2008,512]{1,0:T(8,128)(2,1)S(1)}, u32[]{:S(2)}, u32[]{:S(2)}) collective-permute-start(bf16[2008,512]{1,0:T(8,128)(2,1)} %get-tuple-element.690), channel_id=1, source_target_pairs={{0,15},{1,0},{2,1},{3,2},{4,3},{5,4},{6,5},{7,6},{8,7},{9,8},{10,9... | collective-permute-start | bytes 6168584 | tf_op jit(solution)/shard_map/while/body/eval_jaxpr/ppermute | solution.py:59
  612.6 7.3 copy-start.5
  619.8 79.1 %collective-permute-start.2 = (f32[2008,512]{1,0:T(8,128)}, f32[2008,512]{1,0:T(8,128)}, u32[]{:S(2)}, u32[]{:S(2)}) collective-permute-start(f32[2008,512]{1,0:T(8,128)} %get-tuple-element.691), channel_id=1, source_target_pairs={{0,15},{1,0},{2,1},{3,2},{4,3},{5,4},{6,5},{7,6},{8,7},{9,8},{10,9... | collective-permute-start | bytes 12337160 | tf_op jit(solution)/shard_map/while/body/eval_jaxpr/ppermute | solution.py:60
  624.5 67.2 %collective-permute-start.1 = (bf16[2008,512]{1,0:T(8,128)(2,1)}, bf16[2008,512]{1,0:T(8,128)(2,1)S(1)}, u32[]{:S(2)}, u32[]{:S(2)}) collective-permute-start(bf16[2008,512]{1,0:T(8,128)(2,1)} %get-tuple-element.690), channel_id=1, source_target_pairs={{0,15},{1,0},{2,1},{3,2},{4,3},{5,4},{6,5},{7,6},{8,7},{9,8},{10,9... | collective-permute-start | bytes 6168584 | tf_op jit(solution)/shard_map/while/body/eval_jaxpr/ppermute | solution.py:59
  706.2 79.1 %collective-permute-start.2 = (f32[2008,512]{1,0:T(8,128)}, f32[2008,512]{1,0:T(8,128)}, u32[]{:S(2)}, u32[]{:S(2)}) collective-permute-start(f32[2008,512]{1,0:T(8,128)} %get-tuple-element.691), channel_id=1, source_target_pairs={{0,15},{1,0},{2,1},{3,2},{4,3},{5,4},{6,5},{7,6},{8,7},{9,8},{10,9... | collective-permute-start | bytes 12337160 | tf_op jit(solution)/shard_map/while/body/eval_jaxpr/ppermute | solution.py:60
  710.8 67.2 %collective-permute-start.1 = (bf16[2008,512]{1,0:T(8,128)(2,1)}, bf16[2008,512]{1,0:T(8,128)(2,1)S(1)}, u32[]{:S(2)}, u32[]{:S(2)}) collective-permute-start(bf16[2008,512]{1,0:T(8,128)(2,1)} %get-tuple-element.690), channel_id=1, source_target_pairs={{0,15},{1,0},{2,1},{3,2},{4,3},{5,4},{6,5},{7,6},{8,7},{9,8},{10,9... | collective-permute-start | bytes 6168584 | tf_op jit(solution)/shard_map/while/body/eval_jaxpr/ppermute | solution.py:59
  792.5 79.1 %collective-permute-start.2 = (f32[2008,512]{1,0:T(8,128)}, f32[2008,512]{1,0:T(8,128)}, u32[]{:S(2)}, u32[]{:S(2)}) collective-permute-start(f32[2008,512]{1,0:T(8,128)} %get-tuple-element.691), channel_id=1, source_target_pairs={{0,15},{1,0},{2,1},{3,2},{4,3},{5,4},{6,5},{7,6},{8,7},{9,8},{10,9... | collective-permute-start | bytes 12337160 | tf_op jit(solution)/shard_map/while/body/eval_jaxpr/ppermute | solution.py:60
  797.1 67.2 %collective-permute-start.1 = (bf16[2008,512]{1,0:T(8,128)(2,1)}, bf16[2008,512]{1,0:T(8,128)(2,1)S(1)}, u32[]{:S(2)}, u32[]{:S(2)}) collective-permute-start(bf16[2008,512]{1,0:T(8,128)(2,1)} %get-tuple-element.690), channel_id=1, source_target_pairs={{0,15},{1,0},{2,1},{3,2},{4,3},{5,4},{6,5},{7,6},{8,7},{9,8},{10,9... | collective-permute-start | bytes 6168584 | tf_op jit(solution)/shard_map/while/body/eval_jaxpr/ppermute | solution.py:59
  878.8 79.1 %collective-permute-start.2 = (f32[2008,512]{1,0:T(8,128)}, f32[2008,512]{1,0:T(8,128)}, u32[]{:S(2)}, u32[]{:S(2)}) collective-permute-start(f32[2008,512]{1,0:T(8,128)} %get-tuple-element.691), channel_id=1, source_target_pairs={{0,15},{1,0},{2,1},{3,2},{4,3},{5,4},{6,5},{7,6},{8,7},{9,8},{10,9... | collective-permute-start | bytes 12337160 | tf_op jit(solution)/shard_map/while/body/eval_jaxpr/ppermute | solution.py:60
  883.5 67.2 %collective-permute-start.1 = (bf16[2008,512]{1,0:T(8,128)(2,1)}, bf16[2008,512]{1,0:T(8,128)(2,1)S(1)}, u32[]{:S(2)}, u32[]{:S(2)}) collective-permute-start(bf16[2008,512]{1,0:T(8,128)(2,1)} %get-tuple-element.690), channel_id=1, source_target_pairs={{0,15},{1,0},{2,1},{3,2},{4,3},{5,4},{6,5},{7,6},{8,7},{9,8},{10,9... | collective-permute-start | bytes 6168584 | tf_op jit(solution)/shard_map/while/body/eval_jaxpr/ppermute | solution.py:59
  965.2 79.1 %collective-permute-start.2 = (f32[2008,512]{1,0:T(8,128)}, f32[2008,512]{1,0:T(8,128)}, u32[]{:S(2)}, u32[]{:S(2)}) collective-permute-start(f32[2008,512]{1,0:T(8,128)} %get-tuple-element.691), channel_id=1, source_target_pairs={{0,15},{1,0},{2,1},{3,2},{4,3},{5,4},{6,5},{7,6},{8,7},{9,8},{10,9... | collective-permute-start | bytes 12337160 | tf_op jit(solution)/shard_map/while/body/eval_jaxpr/ppermute | solution.py:60
  969.8 67.2 %collective-permute-start.1 = (bf16[2008,512]{1,0:T(8,128)(2,1)}, bf16[2008,512]{1,0:T(8,128)(2,1)S(1)}, u32[]{:S(2)}, u32[]{:S(2)}) collective-permute-start(bf16[2008,512]{1,0:T(8,128)(2,1)} %get-tuple-element.690), channel_id=1, source_target_pairs={{0,15},{1,0},{2,1},{3,2},{4,3},{5,4},{6,5},{7,6},{8,7},{9,8},{10,9... | collective-permute-start | bytes 6168584 | tf_op jit(solution)/shard_map/while/body/eval_jaxpr/ppermute | solution.py:59
  1051.5 79.1 %collective-permute-start.2 = (f32[2008,512]{1,0:T(8,128)}, f32[2008,512]{1,0:T(8,128)}, u32[]{:S(2)}, u32[]{:S(2)}) collective-permute-start(f32[2008,512]{1,0:T(8,128)} %get-tuple-element.691), channel_id=1, source_target_pairs={{0,15},{1,0},{2,1},{3,2},{4,3},{5,4},{6,5},{7,6},{8,7},{9,8},{10,9... | collective-permute-start | bytes 12337160 | tf_op jit(solution)/shard_map/while/body/eval_jaxpr/ppermute | solution.py:60
  1056.1 67.2 %collective-permute-start.1 = (bf16[2008,512]{1,0:T(8,128)(2,1)}, bf16[2008,512]{1,0:T(8,128)(2,1)S(1)}, u32[]{:S(2)}, u32[]{:S(2)}) collective-permute-start(bf16[2008,512]{1,0:T(8,128)(2,1)} %get-tuple-element.690), channel_id=1, source_target_pairs={{0,15},{1,0},{2,1},{3,2},{4,3},{5,4},{6,5},{7,6},{8,7},{9,8},{10,9... | collective-permute-start | bytes 6168584 | tf_op jit(solution)/shard_map/while/body/eval_jaxpr/ppermute | solution.py:59
  1137.8 79.1 %collective-permute-start.2 = (f32[2008,512]{1,0:T(8,128)}, f32[2008,512]{1,0:T(8,128)}, u32[]{:S(2)}, u32[]{:S(2)}) collective-permute-start(f32[2008,512]{1,0:T(8,128)} %get-tuple-element.691), channel_id=1, source_target_pairs={{0,15},{1,0},{2,1},{3,2},{4,3},{5,4},{6,5},{7,6},{8,7},{9,8},{10,9... | collective-permute-start | bytes 12337160 | tf_op jit(solution)/shard_map/while/body/eval_jaxpr/ppermute | solution.py:60
  1142.5 67.2 %collective-permute-start.1 = (bf16[2008,512]{1,0:T(8,128)(2,1)}, bf16[2008,512]{1,0:T(8,128)(2,1)S(1)}, u32[]{:S(2)}, u32[]{:S(2)}) collective-permute-start(bf16[2008,512]{1,0:T(8,128)(2,1)} %get-tuple-element.690), channel_id=1, source_target_pairs={{0,15},{1,0},{2,1},{3,2},{4,3},{5,4},{6,5},{7,6},{8,7},{9,8},{10,9... | collective-permute-start | bytes 6168584 | tf_op jit(solution)/shard_map/while/body/eval_jaxpr/ppermute | solution.py:59
  1224.2 79.1 %collective-permute-start.2 = (f32[2008,512]{1,0:T(8,128)}, f32[2008,512]{1,0:T(8,128)}, u32[]{:S(2)}, u32[]{:S(2)}) collective-permute-start(f32[2008,512]{1,0:T(8,128)} %get-tuple-element.691), channel_id=1, source_target_pairs={{0,15},{1,0},{2,1},{3,2},{4,3},{5,4},{6,5},{7,6},{8,7},{9,8},{10,9... | collective-permute-start | bytes 12337160 | tf_op jit(solution)/shard_map/while/body/eval_jaxpr/ppermute | solution.py:60
  1228.8 67.2 %collective-permute-start.1 = (bf16[2008,512]{1,0:T(8,128)(2,1)}, bf16[2008,512]{1,0:T(8,128)(2,1)S(1)}, u32[]{:S(2)}, u32[]{:S(2)}) collective-permute-start(bf16[2008,512]{1,0:T(8,128)(2,1)} %get-tuple-element.690), channel_id=1, source_target_pairs={{0,15},{1,0},{2,1},{3,2},{4,3},{5,4},{6,5},{7,6},{8,7},{9,8},{10,9... | collective-permute-start | bytes 6168584 | tf_op jit(solution)/shard_map/while/body/eval_jaxpr/ppermute | solution.py:59
  1310.5 79.1 %collective-permute-start.2 = (f32[2008,512]{1,0:T(8,128)}, f32[2008,512]{1,0:T(8,128)}, u32[]{:S(2)}, u32[]{:S(2)}) collective-permute-start(f32[2008,512]{1,0:T(8,128)} %get-tuple-element.691), channel_id=1, source_target_pairs={{0,15},{1,0},{2,1},{3,2},{4,3},{5,4},{6,5},{7,6},{8,7},{9,8},{10,9... | collective-permute-start | bytes 12337160 | tf_op jit(solution)/shard_map/while/body/eval_jaxpr/ppermute | solution.py:60
  1315.1 67.2 %collective-permute-start.1 = (bf16[2008,512]{1,0:T(8,128)(2,1)}, bf16[2008,512]{1,0:T(8,128)(2,1)S(1)}, u32[]{:S(2)}, u32[]{:S(2)}) collective-permute-start(bf16[2008,512]{1,0:T(8,128)(2,1)} %get-tuple-element.690), channel_id=1, source_target_pairs={{0,15},{1,0},{2,1},{3,2},{4,3},{5,4},{6,5},{7,6},{8,7},{9,8},{10,9... | collective-permute-start | bytes 6168584 | tf_op jit(solution)/shard_map/while/body/eval_jaxpr/ppermute | solution.py:59
  1396.8 79.1 %collective-permute-start.2 = (f32[2008,512]{1,0:T(8,128)}, f32[2008,512]{1,0:T(8,128)}, u32[]{:S(2)}, u32[]{:S(2)}) collective-permute-start(f32[2008,512]{1,0:T(8,128)} %get-tuple-element.691), channel_id=1, source_target_pairs={{0,15},{1,0},{2,1},{3,2},{4,3},{5,4},{6,5},{7,6},{8,7},{9,8},{10,9... | collective-permute-start | bytes 12337160 | tf_op jit(solution)/shard_map/while/body/eval_jaxpr/ppermute | solution.py:60
  1401.5 67.2 %collective-permute-start.1 = (bf16[2008,512]{1,0:T(8,128)(2,1)}, bf16[2008,512]{1,0:T(8,128)(2,1)S(1)}, u32[]{:S(2)}, u32[]{:S(2)}) collective-permute-start(bf16[2008,512]{1,0:T(8,128)(2,1)} %get-tuple-element.690), channel_id=1, source_target_pairs={{0,15},{1,0},{2,1},{3,2},{4,3},{5,4},{6,5},{7,6},{8,7},{9,8},{10,9... | collective-permute-start | bytes 6168584 | tf_op jit(solution)/shard_map/while/body/eval_jaxpr/ppermute | solution.py:59
  1483.2 79.1 %collective-permute-start.2 = (f32[2008,512]{1,0:T(8,128)}, f32[2008,512]{1,0:T(8,128)}, u32[]{:S(2)}, u32[]{:S(2)}) collective-permute-start(f32[2008,512]{1,0:T(8,128)} %get-tuple-element.691), channel_id=1, source_target_pairs={{0,15},{1,0},{2,1},{3,2},{4,3},{5,4},{6,5},{7,6},{8,7},{9,8},{10,9... | collective-permute-start | bytes 12337160 | tf_op jit(solution)/shard_map/while/body/eval_jaxpr/ppermute | solution.py:60
  1487.8 67.2 %collective-permute-start.1 = (bf16[2008,512]{1,0:T(8,128)(2,1)}, bf16[2008,512]{1,0:T(8,128)(2,1)S(1)}, u32[]{:S(2)}, u32[]{:S(2)}) collective-permute-start(bf16[2008,512]{1,0:T(8,128)(2,1)} %get-tuple-element.690), channel_id=1, source_target_pairs={{0,15},{1,0},{2,1},{3,2},{4,3},{5,4},{6,5},{7,6},{8,7},{9,8},{10,9... | collective-permute-start | bytes 6168584 | tf_op jit(solution)/shard_map/while/body/eval_jaxpr/ppermute | solution.py:59
  1569.5 79.1 %collective-permute-start.2 = (f32[2008,512]{1,0:T(8,128)}, f32[2008,512]{1,0:T(8,128)}, u32[]{:S(2)}, u32[]{:S(2)}) collective-permute-start(f32[2008,512]{1,0:T(8,128)} %get-tuple-element.691), channel_id=1, source_target_pairs={{0,15},{1,0},{2,1},{3,2},{4,3},{5,4},{6,5},{7,6},{8,7},{9,8},{10,9... | collective-permute-start | bytes 12337160 | tf_op jit(solution)/shard_map/while/body/eval_jaxpr/ppermute | solution.py:60
  1574.1 67.2 %collective-permute-start.1 = (bf16[2008,512]{1,0:T(8,128)(2,1)}, bf16[2008,512]{1,0:T(8,128)(2,1)S(1)}, u32[]{:S(2)}, u32[]{:S(2)}) collective-permute-start(bf16[2008,512]{1,0:T(8,128)(2,1)} %get-tuple-element.690), channel_id=1, source_target_pairs={{0,15},{1,0},{2,1},{3,2},{4,3},{5,4},{6,5},{7,6},{8,7},{9,8},{10,9... | collective-permute-start | bytes 6168584 | tf_op jit(solution)/shard_map/while/body/eval_jaxpr/ppermute | solution.py:59
  1655.8 79.1 %collective-permute-start.2 = (f32[2008,512]{1,0:T(8,128)}, f32[2008,512]{1,0:T(8,128)}, u32[]{:S(2)}, u32[]{:S(2)}) collective-permute-start(f32[2008,512]{1,0:T(8,128)} %get-tuple-element.691), channel_id=1, source_target_pairs={{0,15},{1,0},{2,1},{3,2},{4,3},{5,4},{6,5},{7,6},{8,7},{9,8},{10,9... | collective-permute-start | bytes 12337160 | tf_op jit(solution)/shard_map/while/body/eval_jaxpr/ppermute | solution.py:60
  1660.5 67.2 %collective-permute-start.1 = (bf16[2008,512]{1,0:T(8,128)(2,1)}, bf16[2008,512]{1,0:T(8,128)(2,1)S(1)}, u32[]{:S(2)}, u32[]{:S(2)}) collective-permute-start(bf16[2008,512]{1,0:T(8,128)(2,1)} %get-tuple-element.690), channel_id=1, source_target_pairs={{0,15},{1,0},{2,1},{3,2},{4,3},{5,4},{6,5},{7,6},{8,7},{9,8},{10,9... | collective-permute-start | bytes 6168584 | tf_op jit(solution)/shard_map/while/body/eval_jaxpr/ppermute | solution.py:59
  1742.2 79.1 %collective-permute-start.2 = (f32[2008,512]{1,0:T(8,128)}, f32[2008,512]{1,0:T(8,128)}, u32[]{:S(2)}, u32[]{:S(2)}) collective-permute-start(f32[2008,512]{1,0:T(8,128)} %get-tuple-element.691), channel_id=1, source_target_pairs={{0,15},{1,0},{2,1},{3,2},{4,3},{5,4},{6,5},{7,6},{8,7},{9,8},{10,9... | collective-permute-start | bytes 12337160 | tf_op jit(solution)/shard_map/while/body/eval_jaxpr/ppermute | solution.py:60
  1746.8 67.2 %collective-permute-start.1 = (bf16[2008,512]{1,0:T(8,128)(2,1)}, bf16[2008,512]{1,0:T(8,128)(2,1)S(1)}, u32[]{:S(2)}, u32[]{:S(2)}) collective-permute-start(bf16[2008,512]{1,0:T(8,128)(2,1)} %get-tuple-element.690), channel_id=1, source_target_pairs={{0,15},{1,0},{2,1},{3,2},{4,3},{5,4},{6,5},{7,6},{8,7},{9,8},{10,9... | collective-permute-start | bytes 6168584 | tf_op jit(solution)/shard_map/while/body/eval_jaxpr/ppermute | solution.py:59
  1828.5 77.4 %collective-permute-start.3 = (f32[2008,512]{1,0:T(8,128)}, f32[2008,512]{1,0:T(8,128)}, u32[]{:S(2)}, u32[]{:S(2)}) collective-permute-start(f32[2008,512]{1,0:T(8,128)} %get-tuple-element.452), channel_id=1, source_target_pairs={{0,15},{1,0},{2,1},{3,2},{4,3},{5,4},{6,5},{7,6},{8,7},{9,8},{10,9... | collective-permute-start | bytes 12337160 | tf_op jit(solution)/shard_map/ppermute | solution.py:65
  (32 other events, 165.7 us)
where the time goes:
time: 1910 us
  waiting for transfers between devices  1350 us (71%)
  matrix products  250 us (13%)
  starting transfers between devices  145 us (8%)
  blocking collectives  72.7 us (4%)
  local copies, waits for them, and re-layouts  48.3 us (3%)
  other arithmetic  39.2 us (2%)
    ppermute x15, waiting for transfers between devices, bwd_body(): w_cur = lax.ppermute(w_cur, 'fsdp', shift_perm)  1010 us
    ppermute x15, waiting for transfers between devices, fwd_body(): w_cur = lax.ppermute(w_cur, 'fsdp', shift_perm)  346 us
    dot_general x16, matrix products, bwd_update(): lax.dot_general(d_logits, tok_rows, (((0,), (0,)), ((), ())), preferred_e...  113 us
    dot_general x31, matrix products, block_logits(): lax.dot_general(tok_rows, w_blk, (((1,), (1,)), ((), ())), preferred_elem...  93.9 us
    psum x1, blocking collectives, local_head(): lax.psum(jnp.sum((log_norm - tgt_logit).reshape(n_micro, tok_dev), axis=1...  72.7 us
    ppermute x15, starting transfers between devices, fwd_body(): w_cur = lax.ppermute(w_cur, 'fsdp', shift_perm)  70.3 us
    ppermute x15, starting transfers between devices, bwd_body(): d_w_acc = lax.ppermute(d_w_acc, 'fsdp', shift_perm)  69.4 us
    dot_general x16, matrix products, bwd_update(): jnp.dot(d_logits, w_blk, preferred_element_type=jnp.float32)  43.4 us
  transfers between devices with their start and end apart: 46, of which 30 were waited for; matrix products, arithmetic and copies ran while one was open for 6% of the time, Pallas kernels for 0%

commit v1 on v0

v1 whole, which is shorter than its diff:
```python
import functools
import math

import jax
import jax.numpy as jnp
from jax import lax
from jax.experimental import pallas as pl
from jax.experimental.pallas import tpu as pltpu
from jax.sharding import PartitionSpec as P

LOG2E = math.log2(math.e)
LN2 = math.log(2.0)
TILE = 512
LANES = 128
NQ = TILE // LANES
NZ = 4
MESH = pl.DeviceIdType.MESH
NT = (((1,), (1,)), ((), ()))
F32 = jnp.float32


def dot_nt(a, b):
    return lax.dot_general(a, b, NT, preferred_element_type=F32)


def to_column(row):
    return jnp.broadcast_to(row, (LANES, TILE)).T


COUNTS = dict(W1=1, W2=4, W3=4, H=6, Y=3, L=6, A1=2, A2=2, A3=2, G1=2, G2=2, G3=2, R=6, S=5)
FIRST = {}
for _name, _n in COUNTS.items():
    FIRST[_name] = sum(COUNTS[k] for k in FIRST)
N_SEM = sum(COUNTS.values())


def head_kernel(group, valid, tokens, h_hbm, w_hbm, y_ref, loss_o, dh_o, dw_hbm,
                hb, wb, yb, lp, lr, ab, rs, dh, acc, m_st, s_st, z_ref, c_col, y_col, hits, vb, vr,
                send_sem, recv_sem, load_sem):
    me = lax.axis_index('fsdp')
    core = me + 1 - 2 * lax.rem(me, 2)
    yid = lax.rem(me // 2, 2)
    ypeer = me + 2 - 4 * yid
    zpeer = [lax.rem(me + 4 * s, group) for s in range(NZ)]
    lane = lax.broadcasted_iota(jnp.int32, (1, LANES), 1)
    lane_f = lane.astype(F32)

    def copy(name, j, src, dst, to):
        i = FIRST[name] + j
        return pltpu.make_async_remote_copy(src_ref=src, dst_ref=dst, send_sem=send_sem.at[i], recv_sem=recv_sem.at[i],
                                            device_id={'fsdp': to}, device_id_type=MESH)

    def rows(i):
        return pl.ds(i * TILE, TILE)

    w1 = copy('W1', 0, wb.at[0], wb.at[1], core)
    w2 = [copy('W2', i, wb.at[0, rows(i)], wb.at[2, rows(i)], ypeer) for i in range(4)]
    w3 = [copy('W3', i, wb.at[2, rows(i)], wb.at[3, rows(i)], core) for i in range(4)]
    hs = [[None] + [copy('H', 3 * m + k - 1, hb.at[0, m, k - 1], hb.at[0, m, k], zpeer[1]) for k in range(1, NZ)] for m in range(2)]
    ys = [copy('Y', k - 1, y_ref, yb.at[k - 1], zpeer[k]) for k in range(1, NZ)]
    ls = [[copy('L', 3 * m + s - 1, lp.at[m], lr.at[m, s - 1], zpeer[s]) for s in range(1, NZ)] for m in range(2)]
    a1 = [copy('A1', m, ab.at[0, m], ab.at[1, m], core) for m in range(2)]
    a2 = [copy('A2', m, ab.at[0, m], ab.at[2, m], ypeer) for m in range(2)]
    a3 = [copy('A3', m, ab.at[2, m], ab.at[3, m], core) for m in range(2)]
    g1 = [copy('G1', m, hb.at[0, m], hb.at[1, m], core) for m in range(2)]
    g2 = [copy('G2', m, hb.at[0, m], hb.at[2, m], ypeer) for m in range(2)]
    g3 = [copy('G3', m, hb.at[2, m], hb.at[3, m], core) for m in range(2)]
    rr = [[copy('R', 3 * m + j, dh.at[m, j + 1], rs.at[m, j], zpeer[1]) for j in range(3)] for m in range(2)]
    ss = [copy('S', s - 1, vb.at[0], vr.at[s - 1], zpeer[s]) for s in range(1, NZ)]
    ss.append(copy('S', 3, vb.at[1], vr.at[3], core))
    ss.append(copy('S', 4, vb.at[2], vr.at[4], ypeer))
    every = [w1] + w2 + w3 + hs[0][1:] + hs[1][1:] + ys + ls[0] + ls[1] + a1 + a2 + a3 + g1 + g2 + g3 + rr[0] + rr[1] + ss

    loads = [pltpu.make_async_copy(h_hbm.at[m], hb.at[0, m, 0], load_sem.at[m]) for m in range(2)]
    load_w = pltpu.make_async_copy(w_hbm, wb.at[0], load_sem.at[2])
    loads[0].start()
    load_w.start()
    loads[1].start()

    barrier = pltpu.get_barrier_semaphore()
    for peer in (core, ypeer, zpeer[1], zpeer[2], zpeer[3]):
        pl.semaphore_signal(barrier, inc=1, device_id={'fsdp': peer}, device_id_type=MESH)
    m_st[...] = jnp.full(m_st.shape, -jnp.inf, F32)
    s_st[...] = jnp.zeros(s_st.shape, F32)
    lp[...] = jnp.zeros(lp.shape, F32)
    pl.semaphore_wait(barrier, 5)
    loads[0].wait()
    hs[0][1].start()
    load_w.wait()
    for c in w2:
        c.start()
    w1.start()
    for c in ys:
        c.start()
    loads[1].wait()

    def run_stats(n, unit):
        def logits(u, t, slot):
            m, k, p, half = unit(u)
            start = pl.multiple_of((2 * half + t % 2) * TILE, TILE)
            z_ref[slot] = dot_nt(hb[0, m, k], wb[2 * p + t // 2, pl.ds(start, TILE), :])

        def fold(u, t, slot):
            m, k, p, half = unit(u)
            first = (2 * half + t % 2) * TILE
            zs = [z_ref[slot, :, q * LANES:(q + 1) * LANES] for q in range(NQ)]
            if t % 2 == 1:
                zs[-1] = jnp.where(lane + (first + TILE - LANES) < valid, zs[-1], -jnp.inf)
            old_max = m_st[m, k]
            new_max = jnp.maximum(old_max, functools.reduce(jnp.maximum, zs))
            part = functools.reduce(jnp.add, [jnp.exp2((z - new_max) * LOG2E) for z in zs])
            s_st[m, k] = s_st[m, k] * jnp.exp2((old_max - new_max) * LOG2E) + part
            m_st[m, k] = new_max

        logits(0, 0, 0)

        def body(u, carry):
            for t in range(4):
                if t < 3:
                    logits(u, t + 1, (t + 1) % 2)
                else:
                    logits(jnp.minimum(u + 1, n - 1), 0, 0)
                fold(u, t, t % 2)
            return carry
        lax.fori_loop(0, n, body, 0)

    def finalize(m):
        for k in range(NZ):
            m_lane = m_st[m, k]
            m_row = jnp.max(m_lane, axis=1, keepdims=True)
            s_row = jnp.sum(s_st[m, k] * jnp.exp2((m_lane - m_row) * LOG2E), axis=1, keepdims=True)
            lse = m_row + LN2 * jnp.log2(s_row)
            lp[m, k:k + 1, :] = jnp.broadcast_to(lse, (TILE, LANES)).T[0:1]

    def combine(m):
        for k in range(NZ):
            parts = [lp[m, k:k + 1, :]]
            for s in range(1, NZ):
                j = (k - s) % NZ
                parts.append(lr[m, s - 1, j:j + 1, :])
            top = functools.reduce(jnp.maximum, parts)
            total = functools.reduce(jnp.add, [jnp.exp2((x - top) * LOG2E) for x in parts])
            lse = top + LN2 * jnp.log2(total)
            ab[0, m, k:k + 1, :] = lse * LOG2E + math.log2(tokens)
            tgt = y_ref if k == 0 else yb.at[k - 1]
            ab[0, m, NZ + k:NZ + k + 1, :] = tgt[m:m + 1, :]
            if k == 0:
                own = functools.reduce(jnp.add, [lse[:, q * LANES:(q + 1) * LANES] for q in range(NQ)])
                hits[m] = jnp.zeros((8, LANES), F32)
                vb[0, 8 * m:8 * m + 8, :] = jnp.zeros((8, LANES), F32)
                vb[0, 8 * m:8 * m + 1, :] = own

    def share(m):
        for c in (a1[m], a2[m], g1[m], g2[m]):
            c.start()

    w1.wait_recv()
    run_stats(4, lambda u: (u // 2, 0, 0, lax.rem(u, 2)))
    hs[0][1].wait_recv()
    hs[0][2].start()
    run_stats(2, lambda u: (0, 1, 0, u))
    w2[0].wait_recv()
    w3[0].start()
    w2[1].wait_recv()
    w3[1].start()
    hs[0][2].wait_recv()
    hs[0][3].start()
    run_stats(2, lambda u: (0, 2, 0, u))
    w3[0].wait_recv()
    w3[1].wait_recv()
    run_stats(3, lambda u: (0, u, 1, 0))
    w2[2].wait_recv()
    w3[2].start()
    hs[0][3].wait_recv()
    hs[1][1].start()
    run_stats(3, lambda u: (0, 3, u // 2, lax.rem(u, 2)))
    w2[3].wait_recv()
    w3[3].start()
    w3[2].wait_recv()
    w3[3].wait_recv()
    run_stats(4, lambda u: (0, u, 1, 1))
    finalize(0)
    for c in ls[0]:
        c.start()
    run_stats(2, lambda u: (1, 0, 1, u))
    hs[1][1].wait_recv()
    hs[1][2].start()
    for c in ys:
        c.wait_recv()
    for c in ls[0]:
        c.wait_recv()
    combine(0)
    share(0)

    base = [(me + (1 - 2 * lax.rem(me, 2)) * (w % 2) + (2 - 4 * yid) * (w // 2)) * valid for w in range(4)]

    def dh_step(i, carry):
        m = i // 4
        k = lax.rem(i + 1, NZ)
        c_col[...] = to_column(ab[0, m, pl.ds(k, 1), :])
        y_col[...] = to_column(ab[0, m, pl.ds(k + NZ, 1), :])
        tiles = [(w, t) for w in range(4) for t in range(4)]

        def logits(j):
            w, t = tiles[j]
            z_ref[j % 2] = dot_nt(hb[0, m, k], wb[w, rows(t), :])

        logits(0)
        for j, (w, t) in enumerate(tiles):
            if j + 1 < len(tiles):
                logits(j + 1)
            grads = []
            found = None
            for q in range(NQ):
                first = t * TILE + q * LANES
                z = z_ref[j % 2, :, q * LANES:(q + 1) * LANES]
                prob = jnp.exp2(z * LOG2E - c_col[...])
                hit = y_col[...] == lane_f + (base[w] + first).astype(F32)
                grad = prob - jnp.where(hit, 1.0 / tokens, 0.0)
                if first + LANES > valid:
                    grad = jnp.where(lane + first < valid, grad, 0.0)
                grads.append(grad.astype(jnp.bfloat16))
                picked = jnp.where(hit, z, 0.0)
                found = picked if found is None else found + picked
            part = jnp.dot(jnp.concatenate(grads, axis=1), wb[w, rows(t), :], preferred_element_type=F32)
            if j == 0:
                dh[m, k] = part
            else:
                dh[m, k] += part
            hits[m] += jnp.sum(found.reshape(TILE // 8, 8, LANES), axis=0)

        @pl.when(i == 0)
        def _():
            rr[0][0].start()
            hs[1][2].wait_recv()
            hs[1][3].start()

        @pl.when(i == 1)
        def _():
            run_stats(8, lambda u: (1, 1 + u // 4, lax.rem(u, 4) // 2, lax.rem(u, 2)))
            hs[1][3].wait_recv()
            run_stats(4, lambda u: (1, 3, u // 2, lax.rem(u, 2)))
            finalize(1)
            for c in ls[1]:
                c.start()
            rr[0][0].wait_recv()
            dh[0, 2] += rs[0, 0]
            rr[0][1].start()

        @pl.when(i == 2)
        def _():
            for c in ls[1]:
                c.wait_recv()
            combine(1)
            share(1)

        @pl.when(i == 3)
        def _():
            for c in (g2[0], a2[0]):
                c.wait_recv()
            g3[0].start()
            a3[0].start()

        @pl.when(i == 4)
        def _():
            rr[0][1].wait_recv()
            dh[0, 3] += rs[0, 1]
            rr[0][2].start()
            rr[1][0].start()
        return carry

    lax.fori_loop(0, 8, dh_step, 0)

    for m in range(2):
        vb[0, 8 * m:8 * m + 8, :] = vb[0, 8 * m:8 * m + 8, :] - hits[m]
    rr[0][2].wait_recv()
    dh_o[0] = dh[0, 0] + rs[0, 2]
    for c in ss[:3]:
        c.start()
    for c in (g2[1], a2[1]):
        c.wait_recv()
    g3[1].start()
    a3[1].start()
    for c in g1 + a1:
        c.wait_recv()

    acc[...] = jnp.zeros(acc.shape, F32)
    base0 = me * valid
    outs = [pltpu.make_async_copy(acc.at[pl.ds(r * TILE, min(TILE, valid - r * TILE))],
                                  dw_hbm.at[pl.ds(r * TILE, min(TILE, valid - r * TILE))], load_sem.at[3 + r]) for r in range(4)]

    def dw_step(i, carry):
        g = i // 4
        r = lax.rem(i, 4)
        start = pl.multiple_of(r * TILE, TILE)
        row = (lax.broadcasted_iota(jnp.int32, (TILE, LANES), 0) + (base0 + r * TILE)).astype(F32)
        tiles = [(m, k) for m in range(2) for k in range(NZ)]

        def logits(j):
            m, k = tiles[j]
            z_ref[j % 2] = dot_nt(wb[0, pl.ds(start, TILE), :], hb[g, m, k])

        logits(0)
        for j, (m, k) in enumerate(tiles):
            if j + 1 < len(tiles):
                logits(j + 1)
            grads = []
            for q in range(NQ):
                cols = slice(q * LANES, (q + 1) * LANES)
                prob = jnp.exp2(z_ref[j % 2, :, cols] * LOG2E - ab[g, m, k:k + 1, cols])
                hit = ab[g, m, NZ + k:NZ + k + 1, cols] == row
                grads.append((prob - jnp.where(hit, 1.0 / tokens, 0.0)).astype(jnp.bfloat16))
            acc[pl.ds(start, TILE), :] += jnp.dot(jnp.concatenate(grads, axis=1), hb[g, m, k], preferred_element_type=F32)

        @pl.when(i == 3)
        def _():
            for c in ss[:3]:
                c.wait_recv()
            vb[1] = vb[0] + vr[0] + vr[1] + vr[2]
            ss[3].start()
            rr[1][0].wait_recv()
            dh[1, 2] += rs[1, 0]
            rr[1][1].start()

        @pl.when(i == 7)
        def _():
            ss[3].wait_recv()
            vb[2] = vb[1] + vr[3]
            ss[4].start()
            for c in g3 + a3:
                c.wait_recv()

        @pl.when(i == 9)
        def _():
            rr[1][1].wait_recv()
            dh[1, 3] += rs[1, 1]
            rr[1][2].start()

        for rr_i in range(4):
            @pl.when(i == 12 + rr_i)
            def _():
                outs[rr_i].start()
        return carry

    lax.fori_loop(0, 16, dw_step, 0)
    ss[4].wait_recv()
    loss_o[...] = vb[2] + vr[4]
    rr[1][2].wait_recv()
    dh_o[1] = dh[1, 0] + rs[1, 2]
    for c in outs:
        c.wait()
    for c in every:
        c.wait_send()


def solution(mesh):
    group = mesh.shape['fsdp']

    def local_head(hidden, targets, w_loc):
        valid = w_loc.shape[0]
        tokens = hidden.shape[1] * group
        bf = jnp.bfloat16
        w0 = jnp.pad(w_loc, ((0, 2048 - valid), (0, 0)))
        y = jnp.pad(targets.astype(F32), ((0, 6), (0, 0)))
        any_spec = pl.BlockSpec(memory_space=pl.ANY)
        vmem = pl.BlockSpec(memory_space=pltpu.VMEM)
        loss, d_h, d_w = pl.pallas_call(
            functools.partial(head_kernel, group, valid, tokens),
            out_shape=[jax.ShapeDtypeStruct((16, LANES), F32), jax.ShapeDtypeStruct((2, TILE, 512), F32),
                       jax.ShapeDtypeStruct((valid, 512), F32)],
            in_specs=[any_spec, any_spec, vmem],
            out_specs=[vmem, vmem, any_spec],
            scratch_shapes=[
                pltpu.VMEM((4, 2, NZ, TILE, 512), bf),
                pltpu.VMEM((4, 2048, 512), bf),
                pltpu.VMEM((3, 8, TILE), F32),
                pltpu.VMEM((2, 8, TILE), F32),
                pltpu.VMEM((2, 3, 8, TILE), F32),
                pltpu.VMEM((4, 2, 8, TILE), F32),
                pltpu.VMEM((2, 3, TILE, 512), F32),
                pltpu.VMEM((2, NZ, TILE, 512), F32),
                pltpu.VMEM((2048, 512), F32),
                pltpu.VMEM((2, NZ, TILE, LANES), F32),
                pltpu.VMEM((2, NZ, TILE, LANES), F32),
                pltpu.VMEM((2, TILE, TILE), F32),
                pltpu.VMEM((TILE, LANES), F32),
                pltpu.VMEM((TILE, LANES), F32),
                pltpu.VMEM((2, 8, LANES), F32),
                pltpu.VMEM((3, 16, LANES), F32),
                pltpu.VMEM((5, 16, LANES), F32),
                pltpu.SemaphoreType.DMA((N_SEM,)),
                pltpu.SemaphoreType.DMA((N_SEM,)),
                pltpu.SemaphoreType.DMA((7,)),
            ],
            compiler_params=pltpu.CompilerParams(collective_id=0, has_side_effects=True, vmem_limit_bytes=67043328),
        )(hidden, w0, y)
        loss_vals = jnp.sum(loss.reshape(2, 8 * LANES), axis=1) / tokens
        return loss_vals, d_h, d_w

    return jax.shard_map(local_head, mesh=mesh,
                         in_specs=(P(None, ('dp', 'fsdp'), None), P(None, ('dp', 'fsdp')), P('fsdp', None)),
                         out_specs=(P('dp'), P(None, ('dp', 'fsdp'), None), P(('dp', 'fsdp'), None)),
                         check_vma=False)
```

time: 1910 us -> 265 us (0.14)
  waiting for transfers between devices: 1350 us -> 0 us
  Pallas kernels: 0 us -> 253 us
  matrix products: 250 us -> 0 us
  starting transfers between devices: 145 us -> 0 us
  blocking collectives: 72.7 us -> 0 us
  local copies, waits for them, and re-layouts: 48.3 us -> 8.95 us
  other arithmetic: 39.2 us -> 2.14 us
    ppermute x46 -> x0, waiting for transfers between devices: 1350 us -> none  [the longest x15 1010 us: bwd_body(): w_cur = lax.ppermute(w_cur, 'fsdp', shift_perm)]
    pallas_call x0 -> x1, Pallas kernels: none -> 253 us  [local_head(): pl.pallas_call(functools.partial(head_kernel, group, valid, tokens), out_...]
    dot_general x63 -> x0, matrix products: 250 us -> none  [the longest x16 113 us: bwd_update(): lax.dot_general(d_logits, tok_rows, (((0,), (0,)), ((), ())), preferred_e...]
    ppermute x46 -> x0, starting transfers between devices: 145 us -> none  [the longest x15 70.3 us: fwd_body(): w_cur = lax.ppermute(w_cur, 'fsdp', shift_perm)]
    psum x1 -> x0, blocking collectives: 72.7 us -> none  [local_head(): lax.psum(jnp.sum((log_norm - tgt_logit).reshape(n_micro, tok_dev), axis=1...]
    while x105 -> x0, local copies, waits for them, and re-layouts: 40.7 us -> none
    reduce_sum x17 -> x2, other arithmetic: 38.9 us -> 0.93 us  [local_head(): loss_vals = jnp.sum(loss.reshape(2, 8 * LANES), axis=1) / tokens]
  transfers between devices with their start and end apart: 46 -> 0, of which waited for: 30 -> 0; matrix products, arithmetic and copies ran while one was open for 6% -> 0% of each run, Pallas kernels for 0% -> 0%
where the time goes in v1:
time: 265 us
  Pallas kernels  253 us (95%)
  local copies, waits for them, and re-layouts  8.95 us (3%)
    pallas_call x1, Pallas kernels, local_head(): pl.pallas_call(functools.partial(head_kernel, group, valid, tokens), out_...  253 us

profile of v1, /device:TPU:0, one launch (start us, length us, event | category | flops | bytes accessed | tf_op | source)
XLA Modules:
  0.0 264.6 jit_solution(4225275335398614702)
XLA Ops:
  0.6 0.7 convert_element_type.7
  1.3 0.6 pad.9.y_ref
  1.9 3.0 %pad.8.w_hbm = bf16[2048,512]{1,0:T(8,128)(2,1)} pad(bf16[2008,512]{1,0:T(8,128)(2,1)} %param.5, bf16[]{:T(256)} %constant.6.clone.1), padding=0_40x0_0 | pad | bytes 4153346 | tf_op jit(solution)/shard_map/jit(_pad)/pad | solution.py:363
  5.0 252.8 %shard_map.58 = (f32[16,128]{1,0:T(8,128)}, f32[2,512,512]{2,1,0:T(8,128)}, f32[2008,512]{1,0:T(8,128)}) custom-call(bf16[2,512,512]{2,1,0:T(8,128)(2,1)} %h_hbm.1, bf16[2048,512]{1,0:T(8,128)(2,1)} %pad.8.w_hbm, f32[8,512]{1,0:T(8,128)} %pad.9.y_ref), custom_call_target="tpu_custom_call" | custom-call | tf_op jit(solution)/shard_map/pallas_call | solution.py:367
  257.8 0.8 reduce_sum.10
  258.6 0.1 reduce_sum.14
  258.7 0.1 reduce_sum.18
  258.8 0.5 broadcast_multiply_fusion
  259.3 0.0 copy-start
  259.3 3.2 %copy.8 = f32[2,512,512]{2,1,0:T(8,128)} copy(f32[2,512,512]{2,1,0:T(8,128)} %get-tuple-element.13) | data formatting | bytes 4194304
  262.6 0.0 copy-done
  262.6 2.0 copy.9
Async XLA Ops:
  259.3 3.2 %copy-start = (f32[2008,512]{1,0:T(8,128)S(1)}, f32[2008,512]{1,0:T(8,128)}, u32[]{:S(2)}) copy-start(f32[2008,512]{1,0:T(8,128)} %get-tuple-element.14) | copy-start | bytes 12337156

commit v2 on v1

--- a/solution.py
+++ b/solution.py
@@ -16,6 +16,7 @@
 NZ = 4
 MESH = pl.DeviceIdType.MESH
 NT = (((1,), (1,)), ((), ()))
+TN = (((0,), (0,)), ((), ()))
 F32 = jnp.float32
 
 
@@ -27,17 +28,18 @@
     return jnp.broadcast_to(row, (LANES, TILE)).T
 
 
-COUNTS = dict(W1=1, W2=4, W3=4, H=6, Y=3, L=6, A1=2, A2=2, A3=2, G1=2, G2=2, G3=2, R=6, S=5)
+COUNTS = dict(W1=1, W2=2, WX=2, W3=4, H=12, Y=3, L=6, A2=2, A3=2, G2=2, G3=2, R=12, S=5, D=1)
 FIRST = {}
 for _name, _n in COUNTS.items():
     FIRST[_name] = sum(COUNTS[k] for k in FIRST)
 N_SEM = sum(COUNTS.values())
 
 
-def head_kernel(group, valid, tokens, h_hbm, w_hbm, y_ref, loss_o, dh_o, dw_hbm,
-                hb, wb, yb, lp, lr, ab, rs, dh, acc, m_st, s_st, z_ref, c_col, y_col, hits, vb, vr,
+def head_kernel(group, valid, tokens, h_hbm, w_hbm, y_in, loss_o, dh_o, dw_hbm,
+                hb, wb, yb, lp, lr, ab, rs, dh, dwa, dwr, m_st, s_st, z_ref, c_col, y_col, hits, vb, vr,
                 send_sem, recv_sem, load_sem):
     me = lax.axis_index('fsdp')
+    xid = lax.axis_index('dp')
     core = me + 1 - 2 * lax.rem(me, 2)
     yid = lax.rem(me // 2, 2)
     ypeer = me + 2 - 4 * yid
@@ -45,47 +47,75 @@
     lane = lax.broadcasted_iota(jnp.int32, (1, LANES), 1)
     lane_f = lane.astype(F32)
 
-    def copy(name, j, src, dst, to):
+    def copy(name, j, src, dst, to, axis='fsdp'):
         i = FIRST[name] + j
         return pltpu.make_async_remote_copy(src_ref=src, dst_ref=dst, send_sem=send_sem.at[i], recv_sem=recv_sem.at[i],
-                                            device_id={'fsdp': to}, device_id_type=MESH)
+                                            device_id={axis: to}, device_id_type=MESH)
 
     def rows(i):
         return pl.ds(i * TILE, TILE)
 
+    def wrows(half, i):
+        return pl.ds(pl.multiple_of((2 * half + i) * TILE, TILE), TILE)
+
+    def halves(i):
+        return pl.ds(i * (TILE // 2), TILE // 2)
+
+    xpeer = 1 - xid
     w1 = copy('W1', 0, wb.at[0], wb.at[1], core)
-    w2 = [copy('W2', i, wb.at[0, rows(i)], wb.at[2, rows(i)], ypeer) for i in range(4)]
-    w3 = [copy('W3', i, wb.at[2, rows(i)], wb.at[3, rows(i)], core) for i in range(4)]
-    hs = [[None] + [copy('H', 3 * m + k - 1, hb.at[0, m, k - 1], hb.at[0, m, k], zpeer[1]) for k in range(1, NZ)] for m in range(2)]
-    ys = [copy('Y', k - 1, y_ref, yb.at[k - 1], zpeer[k]) for k in range(1, NZ)]
-    ls = [[copy('L', 3 * m + s - 1, lp.at[m], lr.at[m, s - 1], zpeer[s]) for s in range(1, NZ)] for m in range(2)]
-    a1 = [copy('A1', m, ab.at[0, m], ab.at[1, m], core) for m in range(2)]
-    a2 = [copy('A2', m, ab.at[0, m], ab.at[2, m], ypeer) for m in range(2)]
-    a3 = [copy('A3', m, ab.at[2, m], ab.at[3, m], core) for m in range(2)]
-    g1 = [copy('G1', m, hb.at[0, m], hb.at[1, m], core) for m in range(2)]
-    g2 = [copy('G2', m, hb.at[0, m], hb.at[2, m], ypeer) for m in range(2)]
-    g3 = [copy('G3', m, hb.at[2, m], hb.at[3, m], core) for m in range(2)]
-    rr = [[copy('R', 3 * m + j, dh.at[m, j + 1], rs.at[m, j], zpeer[1]) for j in range(3)] for m in range(2)]
-    ss = [copy('S', s - 1, vb.at[0], vr.at[s - 1], zpeer[s]) for s in range(1, NZ)]
+    w2 = [copy('W2', i, wb.at[0, wrows(xid, i)], wb.at[2, wrows(xid, i)], ypeer) for i in range(2)]
+    wx = [copy('WX', i, wb.at[2, wrows(xid, i)], wb.at[2, wrows(xid, i)], xpeer, 'dp') for i in range(2)]
+    w3 = [copy('W3', 2 * e + i, wb.at[2, wrows(half, i)], wb.at[3, wrows(half, i)], core)
+          for e, half in enumerate((xid, xpeer)) for i in range(2)]
+    hs = [[None] + [[copy('H', 6 * m + 2 * (k - 1) + i, hb.at[0, m, k - 1, halves(i)], hb.at[0, m, k, halves(i)], zpeer[1])
+                     for i in range(2)] for k in range(1, NZ)] for m in range(2)]
+    ys = [copy('Y', k - 1, yb.at[0], yb.at[k], zpeer[k]) for k in range(1, NZ)]
+    ls = [[copy('L', 3 * m + j - 1, lp.at[m], lr.at[m, j - 1], zpeer[j]) for j in range(1, NZ)] for m in range(2)]
+    a2 = [copy('A2', m, ab.at[0, m], ab.at[1, m], ypeer) for m in range(2)]
+    a3 = [copy('A3', m, ab.at[1, m], ab.at[2, m], core) for m in range(2)]
+    g2 = [copy('G2', m, hb.at[0, m], hb.at[1, m], ypeer) for m in range(2)]
+    g3 = [copy('G3', m, hb.at[1, m], hb.at[2, m], core) for m in range(2)]
+    rr = [[[copy('R', 6 * m + 2 * j + i, dh.at[m, j + 1, halves(i)], rs.at[m, j, halves(i)], zpeer[1]) for i in range(2)]
+           for j in range(3)] for m in range(2)]
+    ss = [copy('S', j - 1, vb.at[0], vr.at[j - 1], zpeer[j]) for j in range(1, NZ)]
     ss.append(copy('S', 3, vb.at[1], vr.at[3], core))
     ss.append(copy('S', 4, vb.at[2], vr.at[4], ypeer))
-    every = [w1] + w2 + w3 + hs[0][1:] + hs[1][1:] + ys + ls[0] + ls[1] + a1 + a2 + a3 + g1 + g2 + g3 + rr[0] + rr[1] + ss
+    dw_copy = copy('D', 0, dwa.at[1], dwr, core)
+    every = [w1, dw_copy] + w2 + wx + w3 + ys + ls[0] + ls[1] + a2 + a3 + g2 + g3 + ss
+    for m in range(2):
+        every += [c for pair in hs[m][1:] + rr[m] for c in pair]
+
+    def pass_on(m, k, i):
+        hs[m][k][i].wait_recv()
+        if k + 1 < NZ:
+            hs[m][k + 1][i].start()
+
+    def hop(m, j, i):
+        if j > 0:
+            rr[m][j - 1][i].wait_recv()
+            dh[m, j + 1, halves(i), :] += rs[m, j - 1, halves(i), :]
+        rr[m][j][i].start()
 
     loads = [pltpu.make_async_copy(h_hbm.at[m], hb.at[0, m, 0], load_sem.at[m]) for m in range(2)]
-    load_w = pltpu.make_async_copy(w_hbm, wb.at[0], load_sem.at[2])
     loads[0].start()
+    loads[1].start()
+    clear = (valid // 16) * 16
+    wb[0, clear:, :] = jnp.zeros((2048 - clear, 512), jnp.bfloat16)
+    load_w = pltpu.make_async_copy(w_hbm, wb.at[0, pl.ds(0, valid)], load_sem.at[2])
     load_w.start()
-    loads[1].start()
 
     barrier = pltpu.get_barrier_semaphore()
     for peer in (core, ypeer, zpeer[1], zpeer[2], zpeer[3]):
         pl.semaphore_signal(barrier, inc=1, device_id={'fsdp': peer}, device_id_type=MESH)
+    pl.semaphore_signal(barrier, inc=1, device_id={'dp': xpeer}, device_id_type=MESH)
+    yb[0] = jnp.concatenate([y_in[...].astype(F32), jnp.zeros((6, TILE), F32)], axis=0)
     m_st[...] = jnp.full(m_st.shape, -jnp.inf, F32)
     s_st[...] = jnp.zeros(s_st.shape, F32)
     lp[...] = jnp.zeros(lp.shape, F32)
-    pl.semaphore_wait(barrier, 5)
+    pl.semaphore_wait(barrier, 6)
     loads[0].wait()
-    hs[0][1].start()
+    for i in range(2):
+        hs[0][1][i].start()
     load_w.wait()
     for c in w2:
         c.start()
@@ -142,55 +172,55 @@
             total = functools.reduce(jnp.add, [jnp.exp2((x - top) * LOG2E) for x in parts])
             lse = top + LN2 * jnp.log2(total)
             ab[0, m, k:k + 1, :] = lse * LOG2E + math.log2(tokens)
-            tgt = y_ref if k == 0 else yb.at[k - 1]
-            ab[0, m, NZ + k:NZ + k + 1, :] = tgt[m:m + 1, :]
+            ab[0, m, NZ + k:NZ + k + 1, :] = yb[k, m:m + 1, :]
             if k == 0:
                 own = functools.reduce(jnp.add, [lse[:, q * LANES:(q + 1) * LANES] for q in range(NQ)])
                 hits[m] = jnp.zeros((8, LANES), F32)
                 vb[0, 8 * m:8 * m + 8, :] = jnp.zeros((8, LANES), F32)
                 vb[0, 8 * m:8 * m + 1, :] = own
 
-    def share(m):
-        for c in (a1[m], a2[m], g1[m], g2[m]):
-            c.start()
-
     w1.wait_recv()
     run_stats(4, lambda u: (u // 2, 0, 0, lax.rem(u, 2)))
-    hs[0][1].wait_recv()
-    hs[0][2].start()
+    pass_on(0, 1, 0)
+    pass_on(0, 1, 1)
+    w2[0].wait_recv()
+    wx[0].start()
+    w3[0].start()
     run_stats(2, lambda u: (0, 1, 0, u))
-    w2[0].wait_recv()
-    w3[0].start()
+    pass_on(0, 2, 0)
     w2[1].wait_recv()
+    wx[1].start()
     w3[1].start()
-    hs[0][2].wait_recv()
-    hs[0][3].start()
+    pass_on(0, 2, 1)
     run_stats(2, lambda u: (0, 2, 0, u))
+    wx[0].wait_recv()
+    w3[2].start()
     w3[0].wait_recv()
     w3[1].wait_recv()
-    run_stats(3, lambda u: (0, u, 1, 0))
-    w2[2].wait_recv()
-    w3[2].start()
-    hs[0][3].wait_recv()
-    hs[1][1].start()
-    run_stats(3, lambda u: (0, 3, u // 2, lax.rem(u, 2)))
-    w2[3].wait_recv()
+    run_stats(3, lambda u: (0, u, 1, xid))
+    for i in range(2):
+        pass_on(0, 3, i)
+        hs[1][1][i].start()
+    g2[0].start()
+    run_stats(3, lambda u: (0, 3, u // 2, jnp.where(u == 2, xid, lax.rem(u, 2))))
+    wx[1].wait_recv()
     w3[3].start()
     w3[2].wait_recv()
     w3[3].wait_recv()
-    run_stats(4, lambda u: (0, u, 1, 1))
+    run_stats(4, lambda u: (0, u, 1, xpeer))
     finalize(0)
     for c in ls[0]:
         c.start()
+    pass_on(1, 1, 0)
     run_stats(2, lambda u: (1, 0, 1, u))
-    hs[1][1].wait_recv()
-    hs[1][2].start()
+    pass_on(1, 1, 1)
     for c in ys:
         c.wait_recv()
     for c in ls[0]:
         c.wait_recv()
     combine(0)
-    share(0)
+    a2[0].start()
+    dwa[...] = jnp.zeros(dwa.shape, F32)
 
     base = [(me + (1 - 2 * lax.rem(me, 2)) * (w % 2) + (2 - 4 * yid) * (w // 2)) * valid for w in range(4)]
 
@@ -222,75 +252,84 @@
                 grads.append(grad.astype(jnp.bfloat16))
                 picked = jnp.where(hit, z, 0.0)
                 found = picked if found is None else found + picked
-            part = jnp.dot(jnp.concatenate(grads, axis=1), wb[w, rows(t), :], preferred_element_type=F32)
+            grad_tile = jnp.concatenate(grads, axis=1)
+            part = jnp.dot(grad_tile, wb[w, rows(t), :], preferred_element_type=F32)
             if j == 0:
                 dh[m, k] = part
             else:
                 dh[m, k] += part
+            if w < 2:
+                dwa[w, rows(t), :] += lax.dot_general(grad_tile, hb[0, m, k], TN, preferred_element_type=F32)
             hits[m] += jnp.sum(found.reshape(TILE // 8, 8, LANES), axis=0)
 
         @pl.when(i == 0)
         def _():
-            rr[0][0].start()
-            hs[1][2].wait_recv()
-            hs[1][3].start()
+            pass_on(1, 2, 0)
+            pass_on(1, 2, 1)
+            hop(0, 0, 0)
+            hop(0, 0, 1)
 
         @pl.when(i == 1)
         def _():
             run_stats(8, lambda u: (1, 1 + u // 4, lax.rem(u, 4) // 2, lax.rem(u, 2)))
-            hs[1][3].wait_recv()
+            pass_on(1, 3, 0)
+            pass_on(1, 3, 1)
+            g2[1].start()
             run_stats(4, lambda u: (1, 3, u // 2, lax.rem(u, 2)))
             finalize(1)
             for c in ls[1]:
                 c.start()
-            rr[0][0].wait_recv()
-            dh[0, 2] += rs[0, 0]
-            rr[0][1].start()
+            hop(0, 1, 0)
 
         @pl.when(i == 2)
         def _():
+            hop(0, 1, 1)
             for c in ls[1]:
                 c.wait_recv()
             combine(1)
-            share(1)
-
-        @pl.when(i == 3)
-        def _():
+            a2[1].start()
             for c in (g2[0], a2[0]):
                 c.wait_recv()
             g3[0].start()
             a3[0].start()
 
+        @pl.when(i == 3)
+        def _():
+            hop(0, 2, 0)
+
         @pl.when(i == 4)
         def _():
-            rr[0][1].wait_recv()
-            dh[0, 3] += rs[0, 1]
-            rr[0][2].start()
-            rr[1][0].start()
+            hop(0, 2, 1)
+            hop(1, 0, 0)
+            hop(1, 0, 1)
+
+        @pl.when(i == 6)
+        def _():
+            for c in rr[0][2]:
+                c.wait_recv()
+            dh_o[0] = dh[0, 0] + rs[0, 2]
+            for c in (g2[1], a2[1]):
+                c.wait_recv()
+            g3[1].start()
+            a3[1].start()
+
         return carry
 
     lax.fori_loop(0, 8, dh_step, 0)
 
     for m in range(2):
         vb[0, 8 * m:8 * m + 8, :] = vb[0, 8 * m:8 * m + 8, :] - hits[m]
-    rr[0][2].wait_recv()
-    dh_o[0] = dh[0, 0] + rs[0, 2]
     for c in ss[:3]:
         c.start()
-    for c in (g2[1], a2[1]):
-        c.wait_recv()
-    g3[1].start()
-    a3[1].start()
-    for c in g1 + a1:
-        c.wait_recv()
-
-    acc[...] = jnp.zeros(acc.shape, F32)
+    hop(1, 1, 0)
+    dw_copy.start()
+
     base0 = me * valid
-    outs = [pltpu.make_async_copy(acc.at[pl.ds(r * TILE, min(TILE, valid - r * TILE))],
+    outs = [pltpu.make_async_copy(dwa.at[0, pl.ds(r * TILE, min(TILE, valid - r * TILE))],
                                   dw_hbm.at[pl.ds(r * TILE, min(TILE, valid - r * TILE))], load_sem.at[3 + r]) for r in range(4)]
 
     def dw_step(i, carry):
-        g = i // 4
+        g = 1 + i // 4
         r = lax.rem(i, 4)
         start = pl.multiple_of(r * TILE, TILE)
         row = (lax.broadcasted_iota(jnp.int32, (TILE, LANES), 0) + (base0 + r * TILE)).astype(F32)
@@ -310,42 +349,45 @@
                 prob = jnp.exp2(z_ref[j % 2, :, cols] * LOG2E - ab[g, m, k:k + 1, cols])
                 hit = ab[g, m, NZ + k:NZ + k + 1, cols] == row
                 grads.append((prob - jnp.where(hit, 1.0 / tokens, 0.0)).astype(jnp.bfloat16))
-            acc[pl.ds(start, TILE), :] += jnp.dot(jnp.concatenate(grads, axis=1), hb[g, m, k], preferred_element_type=F32)
-
-        @pl.when(i == 3)
+            dwa[0, pl.ds(start, TILE), :] += jnp.dot(jnp.concatenate(grads, axis=1), hb[g, m, k], preferred_element_type=F32)
+
+        @pl.when(i == 1)
         def _():
             for c in ss[:3]:
                 c.wait_recv()
             vb[1] = vb[0] + vr[0] + vr[1] + vr[2]
             ss[3].start()
-            rr[1][0].wait_recv()
-            dh[1, 2] += rs[1, 0]
-            rr[1][1].start()
-
-        @pl.when(i == 7)
+            hop(1, 1, 1)
+
+        @pl.when(i == 4)
+        def _():
+            hop(1, 2, 0)
+
+        @pl.when(i == 6)
+        def _():
+            hop(1, 2, 1)
+
+        @pl.when(i == 3)
         def _():
             ss[3].wait_recv()
             vb[2] = vb[1] + vr[3]
             ss[4].start()
+            dw_copy.wait_recv()
             for c in g3 + a3:
                 c.wait_recv()
 
-        @pl.when(i == 9)
-        def _():
-            rr[1][1].wait_recv()
-            dh[1, 3] += rs[1, 1]
-            rr[1][2].start()
-
-        for rr_i in range(4):
-            @pl.when(i == 12 + rr_i)
+        for r_out in range(4):
+            @pl.when(i == 4 + r_out)
             def _():
-                outs[rr_i].start()
+                dwa[0, rows(r_out), :] += dwr[rows(r_out), :]
+                outs[r_out].start()
         return carry
 
-    lax.fori_loop(0, 16, dw_step, 0)
+    lax.fori_loop(0, 8, dw_step, 0)
     ss[4].wait_recv()
     loss_o[...] = vb[2] + vr[4]
-    rr[1][2].wait_recv()
+    for c in rr[1][2]:
+        c.wait_recv()
     dh_o[1] = dh[1, 0] + rs[1, 2]
     for c in outs:
         c.wait()
@@ -360,8 +402,6 @@
         valid = w_loc.shape[0]
         tokens = hidden.shape[1] * group
         bf = jnp.bfloat16
-        w0 = jnp.pad(w_loc, ((0, 2048 - valid), (0, 0)))
-        y = jnp.pad(targets.astype(F32), ((0, 6), (0, 0)))
         any_spec = pl.BlockSpec(memory_space=pl.ANY)
         vmem = pl.BlockSpec(memory_space=pltpu.VMEM)
         loss, d_h, d_w = pl.pallas_call(
@@ -371,14 +411,15 @@
             in_specs=[any_spec, any_spec, vmem],
             out_specs=[vmem, vmem, any_spec],
             scratch_shapes=[
-                pltpu.VMEM((4, 2, NZ, TILE, 512), bf),
+                pltpu.VMEM((3, 2, NZ, TILE, 512), bf),
                 pltpu.VMEM((4, 2048, 512), bf),
-                pltpu.VMEM((3, 8, TILE), F32),
+                pltpu.VMEM((NZ, 8, TILE), F32),
                 pltpu.VMEM((2, 8, TILE), F32),
                 pltpu.VMEM((2, 3, 8, TILE), F32),
-                pltpu.VMEM((4, 2, 8, TILE), F32),
+                pltpu.VMEM((3, 2, 8, TILE), F32),
                 pltpu.VMEM((2, 3, TILE, 512), F32),
                 pltpu.VMEM((2, NZ, TILE, 512), F32),
+                pltpu.VMEM((2, 2048, 512), F32),
                 pltpu.VMEM((2048, 512), F32),
                 pltpu.VMEM((2, NZ, TILE, LANES), F32),
                 pltpu.VMEM((2, NZ, TILE, LANES), F32),
@@ -393,7 +434,7 @@
                 pltpu.SemaphoreType.DMA((7,)),
             ],
             compiler_params=pltpu.CompilerParams(collective_id=0, has_side_effects=True, vmem_limit_bytes=67043328),
-        )(hidden, w0, y)
+        )(hidden, w_loc, targets)
         loss_vals = jnp.sum(loss.reshape(2, 8 * LANES), axis=1) / tokens
         return loss_vals, d_h, d_w
 

time: 265 us -> 250 us (0.943)
  Pallas kernels: 253 us -> 242 us
  local copies, waits for them, and re-layouts: 8.95 us -> 5.31 us
    pallas_call x1, Pallas kernels: 253 us -> 242 us  [local_head(): pl.pallas_call(functools.partial(head_kernel, group, valid, tokens), out_...]
    pad x2 -> x0, local copies, waits for them, and re-layouts: 3.64 us -> none  [the longest x1 3.03 us: local_head(): w0 = jnp.pad(w_loc, ((0, 2048 - valid), (0, 0)))]
where the time goes in v2:
time: 250 us
  Pallas kernels  242 us (97%)
  local copies, waits for them, and re-layouts  5.31 us (2%)
    pallas_call x1, Pallas kernels, local_head(): pl.pallas_call(functools.partial(head_kernel, group, valid, tokens), out_...  242 us
    unnamed x4, local copies, waits for them, and re-layouts  5.23 us

profile of v2, /device:TPU:0, one launch (start us, length us, event | category | flops | bytes accessed | tf_op | source)
XLA Modules:
  0.0 249.5 jit_solution(15169921201741834845)
XLA Ops:
  0.6 242.1 %shard_map.58 = (f32[16,128]{1,0:T(8,128)}, f32[2,512,512]{2,1,0:T(8,128)}, f32[2008,512]{1,0:T(8,128)}) custom-call(bf16[2,512,512]{2,1,0:T(8,128)(2,1)} %h_hbm.1, bf16[2008,512]{1,0:T(8,128)(2,1)} %w_hbm.1, s32[2,512]{1,0:T(2,128)} %y_in.1), custom_call_target="tpu_custom_call" | custom-call | tf_op jit(solution)/shard_map/pallas_call | solution.py:407
  242.7 0.8 reduce_sum.10
  243.6 0.1 reduce_sum.14
  243.6 0.1 reduce_sum.18
  243.8 0.5 broadcast_multiply_fusion
  244.3 0.0 copy-start
  244.3 3.2 %copy.8 = f32[2,512,512]{2,1,0:T(8,128)} copy(f32[2,512,512]{2,1,0:T(8,128)} %get-tuple-element.13) | data formatting | bytes 4194304
  247.5 0.0 copy-done
  247.5 2.0 copy.9
Async XLA Ops:
  244.3 3.2 %copy-start = (f32[2008,512]{1,0:T(8,128)S(1)}, f32[2008,512]{1,0:T(8,128)}, u32[]{:S(2)}) copy-start(f32[2008,512]{1,0:T(8,128)} %get-tuple-element.14) | copy-start | bytes 12337156
